TPU v7x, 32 devices: a whole 2x2x4 slice. The times are simulated.
32 devices in a mesh: field: 2 (over x), ep: 16 (over z, y, core).
Axes of the slice: x: 2, y: 2, z: 4, core: 2. Of those that a mesh axis runs over, the one named last changes fastest.
Arguments:
- images: float32 [64, 16, 256], P(('field', 'ep')), parts along dimension 0, may hold values from -6 to 6
- reference_image: float32 [32, 256], P('field'), parts along dimension 0, may hold values from -6 to 6
- kernels: float32 [16, 23, 23], replicated, may hold values from -0.25 to 0.25
- kernel_index: int32 [64], P(('field', 'ep')), parts along dimension 0, may hold values from 0 to 15
- tile_mask: int32 [64, 16, 2], P(('field', 'ep')), parts along dimension 0, may hold values 0 or 1
- systematics: float32 [64, 40], P('field'), parts along dimension 0, may hold values from -6 to 6
- onsets: int32 [16], P('field'), parts along dimension 0, may hold values from 0 to 27
Outputs:
- coefficients: float32 [48, 32, 256], P(None, ('field', 'ep')), parts along dimension 1
- epoch_scatter: float32 [64], P('field'), parts along dimension 0
There are 2 independent parts, one for each index of `field`. A program takes and returns all parts, laid end to end along the dimension named above; an argument that names none is the same for every part. Nothing has to cross between parts.
All inputs are finite; a program needn't handle non-finite values. No bound on the sum of `tile_mask` on one device may be relied on, other than what follows from the above.
Results may differ from a plain program's by a relative error of at most 0.00011.
Values sent between devices are 32-bit elements; how exact they have to be, the bound alone decides.
No kernel may reach another device: no remote copies, remote signals or barrier semaphores. Data moves between devices by JAX's collectives and lax.ppermute only.
A program may use at most 64 MiB of HBM per device.

v0:
```python
import math

import jax
import jax.numpy as jnp
from jax import lax
from jax.sharding import PartitionSpec as P

cov_ridge = 0.5
fit_ridge = 1.0


def correlate(stack, chosen):
    count, rows, width = stack.shape
    side = chosen.shape[1]
    half = (side - 1) // 2
    padded = jnp.pad(stack, ((0, 0), (half, half), (half, half)))
    filters = jnp.transpose(chosen, (1, 2, 0))[:, :, None, :]
    strip = math.gcd(rows, 16)

    def one_strip(start):
        piece = lax.dynamic_slice_in_dim(padded, start, strip + 2 * half, 1)
        result = lax.conv_general_dilated(
            piece[None],
            filters,
            (1, 1),
            "VALID",
            dimension_numbers=("NCHW", "HWIO", "NCHW"),
            feature_group_count=count,
            precision=lax.Precision.HIGHEST,
        )
        return result[0]

    starts = jnp.arange(rows // strip, dtype=jnp.int32) * strip
    strips = lax.map(one_strip, starts)
    return jnp.transpose(strips, (1, 0, 2, 3)).reshape(count, rows, width)


def subtract(stack, reference_image, chosen, masks):
    result = reference_image[None] - correlate(stack, chosen)
    shape = result.shape
    tiles = result.reshape(shape[0], shape[1], shape[2] // 128, 128) * masks[..., None].astype(
        jnp.float32
    )
    return tiles.reshape(shape)


def build_design(systematics, onsets):
    count = systematics.shape[0]
    templates = onsets.shape[0]
    epoch_axis = jnp.arange(count, dtype=jnp.float32)[:, None]
    delays = epoch_axis - onsets[None, :].astype(jnp.float32)
    timescale = (jnp.arange(templates, dtype=jnp.float32) + 1.0) * count / (2.0 * templates)
    transient = jnp.where(
        delays >= 0.0, jnp.exp(-jnp.maximum(delays, 0.0) / timescale[None, :]), 0.0
    )
    return jnp.concatenate([systematics, transient], axis=1)


def fit_matrix(scatter, npixels, design):
    count = design.shape[0]
    columns = design.shape[1]
    covariance = scatter / npixels + cov_ridge * jnp.eye(count, dtype=scatter.dtype)
    lower = jnp.linalg.cholesky(covariance)
    weighted = jax.scipy.linalg.cho_solve((lower, True), design)
    normal = jnp.dot(design.T, weighted, precision=lax.Precision.HIGHEST) + fit_ridge * jnp.eye(
        columns, dtype=scatter.dtype
    )
    lower_fit = jnp.linalg.cholesky(normal)
    return jax.scipy.linalg.cho_solve((lower_fit, True), weighted.T)


def shards(images, reference_image, kernels, kernel_index, tile_mask, systematics, onsets):
    local_count, rows, width = images.shape
    basis = kernels.shape[0]
    side = kernels.shape[1]
    onehot = (kernel_index[:, None] == jnp.arange(basis, dtype=jnp.int32)[None, :]).astype(
        jnp.float32
    )
    chosen = jnp.dot(
        onehot, kernels.reshape(basis, side * side), precision=lax.Precision.HIGHEST
    ).reshape(local_count, side, side)
    difference = subtract(images, reference_image, chosen, tile_mask)
    received = lax.all_to_all(difference, "ep", split_axis=1, concat_axis=0, tiled=True)
    count = received.shape[0]
    block_rows = received.shape[1]
    pixel_data = received.reshape(count, block_rows * width)
    partial_value = jnp.dot(pixel_data, pixel_data.T, precision=lax.Precision.HIGHEST)
    scatter = lax.psum(partial_value, "ep")
    npixels = float(rows * width)
    design = build_design(systematics, onsets)
    fit = fit_matrix(scatter, npixels, design)
    coefficients = jnp.dot(fit, pixel_data, precision=lax.Precision.HIGHEST)
    projector = jnp.eye(count, dtype=jnp.float32) - jnp.dot(
        design, fit, precision=lax.Precision.HIGHEST
    )
    product = jnp.dot(projector, scatter, precision=lax.Precision.HIGHEST)
    epoch_scatter = jnp.sum(product * projector, axis=1) / npixels
    return (coefficients.reshape(design.shape[1], block_rows, width), epoch_scatter)


def solution(mesh):
    in_specs = (
        P(("field", "ep"), None, None),
        P("field", None),
        P(),
        P(("field", "ep")),
        P(("field", "ep"), None, None),
        P("field", None),
        P("field"),
    )
    out_specs = (P(None, ("field", "ep"), None), P("field"))
    return jax.shard_map(shards, mesh=mesh, in_specs=in_specs, out_specs=out_specs, check_vma=False)
```

profile of v0, /device:TPU:0, one launch (start us, length us, event | category | flops | bytes accessed | tf_op | source)
XLA Modules:
  0.0 186.9 jit_solution(5411633704186777744)
XLA Ops:
  0.6 0.8 pad_bitcast_fusion
  1.5 0.0 copy-start
  1.5 0.0 copy-start.5
  1.5 0.0 copy-start.4
  1.5 7.8 %copy.30 = f32[1,2,38,278]{1,0,3,2:T(1,128)} copy(f32[1,2,38,278]{3,2,1,0:T(8,128)S(1)} %pad_bitcast_fusion) | data formatting | bytes 169024 | tf_op jit(solution)/shard_map/while/body/eval_jaxpr/broadcast_in_dim | solution.py:23
  9.3 0.0 copy-done
  9.3 0.1 copy.28
  9.3 0.1 reshape.61
  9.5 0.1 dot_general.25
  9.6 0.0 copy-done.5
  9.6 0.2 convolution_bitcast_fusion.1
  9.8 0.3 copy.31
  10.1 0.0 copy-done.4
  10.1 0.7 copy.32
  10.8 0.0 copy-start.2
  10.8 82.8 %fusion.21 = f32[1,2,16,256]{1,0,3,2:T(1,128)S(1)} fusion(f32[1,2,38,278]{1,0,3,2:T(1,128)} %copy.30, f32[23,23,1,2]{3,2,1,0:T(1,128)S(1)} %copy.31), kind=kOutput, calls=%fused_computation.46 | convolution fusion | flops 52002816 | bytes 121512 | tf_op jit(solution)/shard_map/while/body/eval_jaxpr/conv_general_dilated | solution.py:22
  93.6 0.0 copy-done.2
  93.6 0.0 copy-done.3
  93.6 0.9 bitcast_multiply_fusion
  94.5 0.0 copy-start.6
  94.5 0.0 copy-start.1
  94.5 1.2 copy.33
  95.8 7.4 %all-to-all-start = ((f32[2,16,256]{2,0,1:T(2,128)}), f32[2,16,256]{2,0,1:T(2,128)S(1)}, u32[]{:S(2)}, u32[]{:S(2)}) async-start(f32[2,16,256]{2,0,1:T(2,128)} %copy.33), calls=%async_computation | async-start | bytes 65536 | tf_op jit(solution)/shard_map/all_to_all | solution.py:83
  103.2 0.0 copy-done.6
  103.2 6.6 %all-to-all-done = f32[2,16,256]{2,0,1:T(2,128)S(1)} async-done(((f32[2,16,256]{2,0,1:T(2,128)}), f32[2,16,256]{2,0,1:T(2,128)S(1)}, u32[]{:S(2)}, u32[]{:S(2)}) %all-to-all-start) | async-done | bytes 32800 | tf_op jit(solution)/shard_map/all_to_all | solution.py:83
  109.8 0.2 fusion.22
  110.0 57.7 %psum.7 = f32[32,32]{1,0:T(8,128)S(1)} all-reduce(f32[32,32]{1,0:T(8,128)S(1)} %fusion.22), channel_id=1, replica_groups=mesh['field'=2,'ep'=16] {'ep'}, use_global_device_ids=true, to_apply=%region_0.1 | all-reduce | flops 1024 | bytes 8192 | tf_op jit(solution)/shard_map/psum | solution.py:88
  167.7 0.1 copy.34
  167.8 2.9 %cholesky.34 = f32[32,32]{1,0:T(8,128)S(1)} custom-call(f32[32,32]{1,0:T(8,128)S(1)} %fusion.14), custom_call_target="Cholesky" | custom-call | tf_op jit(solution)/shard_map/jit(cholesky)/cholesky | solution.py:63
  170.7 0.6 compare_reduce_fusion.1
  171.4 0.7 fusion.9
  172.0 2.4 %custom-call.20 = f32[1,32,32]{1,2,0:T(8,128)S(1)} custom-call(f32[1,32,32]{2,1,0:T(8,128)S(1)} %fusion.9), custom_call_target="InvertDiagBlocksLowerTriangular" | custom-call | tf_op jit(solution)/shard_map/jit(_cho_solve)/triangular_solve | solution.py:64
  174.4 0.0 copy-done.1
  174.4 0.3 fusion.12
  174.7 0.1 fusion.10
  174.8 0.3 fusion.20
  175.2 0.1 copy.35
  175.3 4.4 %cholesky.64 = f32[48,48]{1,0:T(8,128)S(1)} custom-call(f32[48,48]{1,0:T(8,128)S(1)} %fusion.8), custom_call_target="Cholesky" | custom-call | tf_op jit(solution)/shard_map/jit(cholesky)/cholesky | solution.py:68
  179.7 0.6 compare_reduce_fusion
  180.3 0.7 fusion.2
  181.0 3.7 %custom-call.21 = f32[1,48,48]{1,2,0:T(8,128)S(1)} custom-call(f32[1,48,48]{2,1,0:T(8,128)S(1)} %fusion.2), custom_call_target="InvertDiagBlocksLowerTriangular" | custom-call | tf_op jit(solution)/shard_map/jit(_cho_solve)/triangular_solve | solution.py:69
  184.7 0.2 fusion.5
  184.8 0.2 fusion.3
  185.0 0.2 convolution_subtract_fusion
  185.2 0.2 convolution_bitcast_fusion
  185.5 0.2 fusion
  185.7 0.5 broadcast_multiply_fusion
  186.2 0.7 copy.38
  (11 shorter events, 0.2 us)
Async XLA Ops:
  1.5 7.8 %copy-start = (f32[16,23,23]{2,0,1:T(8,128)S(1)}, f32[16,23,23]{2,0,1:T(8,128)}, u32[]{:S(2)}) copy-start(f32[16,23,23]{2,0,1:T(8,128)} %param.9) | copy-start | bytes 101572
  1.5 8.1 %copy-start.5 = (s32[2]{0:T(128)S(1)}, s32[2]{0:T(128)}, u32[]{:S(2)}) copy-start(s32[2]{0:T(128)} %param.10) | copy-start | bytes 28
  1.5 8.6 %copy-start.4 = (s32[2,16,2]{1,2,0:T(2,128)S(1)}, s32[2,16,2]{1,2,0:T(2,128)}, u32[]{:S(2)}) copy-start(s32[2,16,2]{1,2,0:T(2,128)} %param.11) | copy-start | bytes 772
  10.8 82.8 %copy-start.2 = (f32[2,16,2]{0,2,1:T(2,128)S(1)}, f32[2,16,2]{0,2,1:T(2,128)}, u32[]{:S(2)}) copy-start(f32[2,16,2]{0,2,1:T(2,128)} %copy.32) | copy-start | bytes 772
  10.8 82.8 %copy-start.3 = (f32[16,256]{1,0:T(8,128)S(1)}, f32[16,256]{1,0:T(8,128)}, u32[]{:S(2)}) copy-start(f32[16,256]{1,0:T(8,128)} %param.8) | copy-start | bytes 49156
  94.5 8.7 %copy-start.6 = (s32[8]{0:T(128)S(1)}, s32[8]{0:T(128)}, u32[]{:S(2)}) copy-start(s32[8]{0:T(128)} %param.13) | copy-start | bytes 100
  94.5 79.9 %copy-start.1 = (f32[32,40]{1,0:T(8,128)S(1)}, f32[32,40]{1,0:T(8,128)}, u32[]{:S(2)}) copy-start(f32[32,40]{1,0:T(8,128)} %param.12) | copy-start | bytes 15364
  95.8 14.1 %all-to-all-start = ((f32[2,16,256]{2,0,1:T(2,128)}), f32[2,16,256]{2,0,1:T(2,128)S(1)}, u32[]{:S(2)}, u32[]{:S(2)}) async-start(f32[2,16,256]{2,0,1:T(2,128)} %copy.33), calls=%async_computation | async-start | bytes 65536 | tf_op jit(solution)/shard_map/all_to_all | solution.py:83
where the time goes:
time: 187 us
  matrix products  84.9 us (45%)
  blocking collectives  57.7 us (31%)
  other arithmetic  17.5 us (9%)
  local copies, waits for them, and re-layouts  12 us (6%)
  starting transfers between devices  7.41 us (4%)
  waiting for transfers between devices  6.57 us (4%)
    conv_general_dilated x1, matrix products, one_strip(): lax.conv_general_dilated(piece[None], filters, (1, 1), 'VALID', dimension...  82.8 us
    psum x1, blocking collectives, shards(): scatter = lax.psum(partial_value, 'ep')  57.7 us
    broadcast_in_dim x2, local copies, waits for them, and re-layouts, one_strip(): piece[None]  8.6 us
    all_to_all x1, starting transfers between devices, shards(): lax.all_to_all(difference, 'ep', split_axis=1, concat_axis=0, tiled=True)  7.41 us
    all_to_all x1, waiting for transfers between devices, shards(): lax.all_to_all(difference, 'ep', split_axis=1, concat_axis=0, tiled=True)  6.57 us
    another operation x3, other arithmetic, fit_matrix(): lower_fit = jnp.linalg.cholesky(normal)  5.05 us
    another operation x2, other arithmetic, fit_matrix(): return jax.scipy.linalg.cho_solve((lower_fit, True), weighted.T)  4.32 us
  transfers between devices with their start and end apart: 1, of which 1 were waited for; matrix products, arithmetic and copies ran while one was open for 0% of the time, Pallas kernels for 0%

commit v1 on v0

v1 whole, which is shorter than its diff:
```python
import functools

import jax
import jax.numpy as jnp
from jax import lax
from jax.experimental import pallas as pl
from jax.experimental.pallas import tpu as pltpu
from jax.sharding import PartitionSpec as P

cov_ridge = 0.5
LANES = 128
HI = lax.Precision.HIGHEST


def split(x):
    top = x.astype(jnp.bfloat16)
    return top, (x - top.astype(jnp.float32)).astype(jnp.bfloat16)


def mm(a, b, dims):
    return lax.dot_general(a, b, (dims, ((), ())), preferred_element_type=jnp.float32)


def mm3(a, b, dims):
    a1, a2 = split(a)
    b1, b2 = split(b)
    return mm(a1, b1, dims) + (mm(a1, b2, dims) + mm(a2, b1, dims))


def mmh(a, b, dims):
    return lax.dot_general(
        a, b, (dims, ((), ())), precision=HI, preferred_element_type=jnp.float32
    )


NN = ((1,), (0,))
NT = ((1,), (1,))
TN = ((0,), (0,))


def subtract_kernel(index, images, reference_image, table, masks, out, padded, taps):
    count, rows, width = images.shape
    side = table.shape[0]
    half = (side - 1) // 2
    wide = padded.shape[1]
    per_tile = LANES // rows
    tiles = -(-side // per_tile)
    lane = lax.broadcasted_iota(jnp.int32, (rows, LANES), 1)
    tile_of = lax.broadcasted_iota(jnp.int32, (masks.shape[1], width), 1) // 128
    tile_row = lax.broadcasted_iota(jnp.int32, (masks.shape[1], width), 0)
    spread = (tile_of == tile_row).astype(jnp.float32)
    padded[:, width:] = jnp.zeros((rows, wide - width), jnp.float32)
    for e in range(count):
        chosen = index[e]
        taps[...] = jnp.zeros(taps.shape, jnp.float32)
        for a in range(side):
            taps[a : a + 1, :side] = table[a, pl.ds(chosen, 1), :]
        flipped = pltpu.roll(jnp.transpose(taps[...])[: -(-side // 8) * 8], LANES - half, 1)
        blocks = []
        for t in range(tiles):
            block = jnp.zeros((rows, LANES), jnp.float32)
            for j in range(per_tile):
                b = t * per_tile + j
                if b >= side:
                    continue
                column = jnp.broadcast_to(flipped[b : b + 1, :], (rows, LANES))
                moved = pltpu.roll(
                    column, j * rows, 1, stride=1, stride_axis=0
                )
                here = (lane >= j * rows) & (lane < (j + 1) * rows)
                block = jnp.where(here, moved, block)
            blocks.append(block)
        toeplitz = jnp.concatenate(blocks, axis=1) if tiles > 1 else blocks[0]
        padded[:, :width] = images[e]
        image = padded[...]
        shifted = [
            (pltpu.roll(image, (half - b) % wide, 1) if b != half else image)[:, :width]
            for b in range(side)
        ]
        extra = tiles * per_tile - side
        if extra:
            shifted.append(jnp.zeros((extra * rows, width), jnp.float32))
        stacked = jnp.concatenate(shifted, axis=0)
        model = mm3(toeplitz, stacked, NN)
        good = mm(masks[e].astype(jnp.float32), spread, TN)
        result = (reference_image[...] - model) * good
        for t in range(width // LANES):
            out[e, t] = result[:, t * LANES : (t + 1) * LANES]


def fit_kernel(
    place, near, far, systematics, onsets, coefficients, epoch_scatter, *, rows, order
):
    total = near.shape[0] + far.shape[0]
    count = systematics.shape[0]
    stride = total // count
    width = stride // rows * LANES
    templates = onsets.shape[1]
    npixels = float(rows * width)
    local_bits = (count >> len(order)).bit_length() - 1

    def at(r):
        return jnp.concatenate(
            [half[pl.ds(r, count // 2, stride=stride), :] for half in (near, far)], axis=0
        )

    def true_epoch(here):
        block = here >> local_bits
        flip = jnp.zeros_like(here)
        for b, bit in enumerate(order):
            flip = flip | (((block >> b) & 1) << bit)
        return ((flip ^ place[0]) << local_bits) | (here & ((1 << local_bits) - 1))

    pieces = [at(r) for r in range(stride)]
    pixels = jnp.concatenate(pieces, axis=1)
    top, low = split(pixels)
    first = mm(top, top, NT)
    cross = mm(top, low, NT)
    scatter = first + (cross + jnp.transpose(cross))
    at_row = lax.broadcasted_iota(jnp.int32, (count, count), 0)
    at_col = lax.broadcasted_iota(jnp.int32, (count, count), 1)
    eye = (at_row == at_col).astype(jnp.float32)
    covariance = scatter / npixels + cov_ridge * eye
    epoch = true_epoch(lax.broadcasted_iota(jnp.int32, (count, templates), 0))
    moved = true_epoch(at_row) == at_col
    delays = (epoch - onsets[...]).astype(jnp.float32)
    which = lax.broadcasted_iota(jnp.int32, (count, templates), 1).astype(jnp.float32)
    timescale = (which + 1.0) * (count / (2.0 * templates))
    transient = jnp.where(delays >= 0.0, jnp.exp(-jnp.maximum(delays, 0.0) / timescale), 0.0)
    regressors = mmh(moved.astype(jnp.float32), systematics[...], NN)
    design = jnp.concatenate([regressors, transient], axis=1)
    whole = covariance + mmh(design, design, NT)
    work = jnp.concatenate([whole, eye], axis=1)
    wide_row = lax.broadcasted_iota(jnp.int32, (count, 1), 0)
    for k in range(count):
        column = work[:, k : k + 1]
        pivot = work[k : k + 1, :] / work[k : k + 1, k : k + 1]
        work = jnp.where(wide_row == k, pivot, work - column * pivot)
    inverse = work[:, count:]
    block_rows = rows >> len(order)
    fit = mmh(jnp.transpose(design), inverse, NN)
    for b in range(block_rows):
        line = place[0] * block_rows + b
        chunks = []
        for t in range(0, stride, rows):
            chunk = pieces[t]
            for r in range(1, rows):
                chunk = jnp.where(line == r, pieces[t + r], chunk)
            chunks.append(chunk)
        own = jnp.concatenate(chunks, axis=1)
        coefficients[:, b * width : (b + 1) * width] = mmh(fit, own, NN)
    projector = mmh(covariance, inverse, NN)
    product = mmh(projector, scatter, NN)
    per_epoch = jnp.sum(product * projector, axis=1, keepdims=True) * (1.0 / npixels)
    epoch_scatter[...] = jnp.sum(jnp.where(moved, per_epoch, 0.0), axis=0, keepdims=True)


def shards(images, reference_image, kernels, kernel_index, tile_mask, systematics, onsets):
    local_count, rows, width = images.shape
    side = kernels.shape[1]
    vmem = pl.BlockSpec(memory_space=pltpu.VMEM)
    smem = pl.BlockSpec(memory_space=pltpu.SMEM)
    difference = pl.pallas_call(
        subtract_kernel,
        out_shape=jax.ShapeDtypeStruct((local_count, width // LANES, rows, LANES), jnp.float32),
        in_specs=[smem, vmem, vmem, vmem, vmem],
        out_specs=vmem,
        scratch_shapes=[
            pltpu.VMEM((rows, width + LANES), jnp.float32),
            pltpu.VMEM((LANES, LANES), jnp.float32),
        ],
        name="subtract",
    )(
        kernel_index,
        images,
        reference_image,
        jnp.transpose(kernels, (1, 0, 2)),
        jnp.transpose(tile_mask, (0, 2, 1)),
    )
    count = systematics.shape[0]
    devices = lax.axis_size("ep")
    near, far = gather(difference.reshape(-1, LANES), devices)
    block_rows = rows // devices
    place = lax.axis_index("ep").astype(jnp.int32).reshape(1)
    columns = systematics.shape[1] + onsets.shape[0]
    coefficients, epoch_scatter = pl.pallas_call(
        functools.partial(fit_kernel, rows=rows, order=exchange_order(devices)),
        out_shape=(
            jax.ShapeDtypeStruct((columns, block_rows * width), jnp.float32),
            jax.ShapeDtypeStruct((1, count), jnp.float32),
        ),
        in_specs=[smem, vmem, vmem, vmem, vmem],
        out_specs=(vmem, vmem),
        name="fit",
    )(place, near, far, systematics, onsets.reshape(1, -1))
    return (coefficients.reshape(columns, block_rows, width), epoch_scatter.reshape(count))


def exchange_order(devices):
    bits = devices.bit_length() - 1
    if bits < 2:
        return list(range(bits))
    return [bits - 2, bits - 1] + list(range(bits - 3, -1, -1))


def swap(block, devices, flip):
    return lax.ppermute(block, "ep", [(i, i ^ flip) for i in range(devices)])


def gather(block, devices):
    order = exchange_order(devices)
    if len(order) > 2:
        low, high = 1 << order[0], 1 << order[1]
        parts = [block] + [swap(block, devices, flip) for flip in (low, high, low | high)]
        block = jnp.concatenate(parts, axis=0)
        order = order[2:]
    for bit in order[:-1]:
        block = jnp.concatenate([block, swap(block, devices, 1 << bit)], axis=0)
    return block, swap(block, devices, 1 << order[-1])


def solution(mesh):
    in_specs = (
        P(("field", "ep"), None, None),
        P("field", None),
        P(),
        P(("field", "ep")),
        P(("field", "ep"), None, None),
        P("field", None),
        P("field"),
    )
    out_specs = (P(None, ("field", "ep"), None), P("field"))
    return jax.shard_map(shards, mesh=mesh, in_specs=in_specs, out_specs=out_specs, check_vma=False)
```

time: 187 us -> 29.3 us (0.16)
  matrix products: 84.9 us -> 0 us
  blocking collectives: 57.7 us -> 0 us
  other arithmetic: 17.5 us -> 0.01 us
  local copies, waits for them, and re-layouts: 12 us -> 3.03 us
  Pallas kernels: 0 us -> 7.92 us
  waiting for transfers between devices: 6.57 us -> 10 us
    conv_general_dilated x1 -> x0, matrix products: 82.8 us -> none  [one_strip(): lax.conv_general_dilated(piece[None], filters, (1, 1), 'VALID', dimension...]
    psum x1 -> x0, blocking collectives: 57.7 us -> none  [shards(): scatter = lax.psum(partial_value, 'ep')]
    another operation x10 -> x0, other arithmetic: 16.1 us -> none  [the longest x3 5.05 us: fit_matrix(): lower_fit = jnp.linalg.cholesky(normal)]
    ppermute x0 -> x5, waiting for transfers between devices: none -> 10 us  [swap(): return lax.ppermute(block, 'ep', [(i, i ^ flip) for i in range(devices)])]
    broadcast_in_dim x3 -> x0, local copies, waits for them, and re-layouts: 8.86 us -> none  [the longest x2 8.6 us: one_strip(): piece[None]]
    pallas_call x0 -> x2, Pallas kernels: none -> 7.92 us  [the longest x1 5.51 us: shards(): pl.pallas_call(functools.partial(fit_kernel, rows=rows, order=exchange_or...]
    all_to_all x1 -> x0, starting transfers between devices: 7.41 us -> none  [shards(): lax.all_to_all(difference, 'ep', split_axis=1, concat_axis=0, tiled=True)]
    ppermute x0 -> x5, starting transfers between devices: none -> 7.3 us  [swap(): return lax.ppermute(block, 'ep', [(i, i ^ flip) for i in range(devices)])]
  transfers between devices with their start and end apart: 1 -> 5, of which waited for: 1 -> 4; matrix products, arithmetic and copies ran while one was open for 0% -> 3% of each run, Pallas kernels for 0% -> 0%
where the time goes in v1:
time: 29.3 us; the launch traced here: 29 us
  waiting for transfers between devices  10 us (34%)
  Pallas kernels  7.92 us (27%)
  starting transfers between devices  7.3 us (25%)
  local copies, waits for them, and re-layouts  3.03 us (10%)
  between operations  0.68 us (2%)
    ppermute x5, waiting for transfers between devices, swap(): return lax.ppermute(block, 'ep', [(i, i ^ flip) for i in range(devices)])  10 us
    ppermute x5, starting transfers between devices, swap(): return lax.ppermute(block, 'ep', [(i, i ^ flip) for i in range(devices)])  7.3 us
    pallas_call x1, Pallas kernels, shards(): pl.pallas_call(functools.partial(fit_kernel, rows=rows, order=exchange_or...  5.51 us
    unnamed x11, local copies, waits for them, and re-layouts  3.02 us
    pallas_call x1, Pallas kernels, shards(): pl.pallas_call(subtract_kernel, out_shape=jax.ShapeDtypeStruct((local_cou...  2.4 us
  transfers between devices with their start and end apart: 5, of which 4 were waited for; matrix products, arithmetic and copies ran while one was open for 3% of the time, Pallas kernels for 0%

profile of v1, /device:TPU:0, one launch (start us, length us, event | category | flops | bytes accessed | tf_op | source)
XLA Modules:
  0.0 29.0 jit_solution(3832015981513462512)
XLA Ops:
  0.6 2.4 %subtract.1 = f32[2,2,16,128]{3,2,1,0:T(8,128)} custom-call(s32[2]{0:T(128)} %index.1, f32[2,16,256]{2,1,0:T(8,128)} %images.1, f32[16,256]{1,0:T(8,128)} %reference_image.1, f32[23,16,23]{2,1,0:T(8,128)} %bitcast.12, s32[2,2,16]{2,1,0:T(2,128)} %bitcast.14), custom_call_target="tpu_custom_call" | custom-call | tf_op jit(solution)/shard_map/subtract/pallas_call | solution.py:163
  3.0 0.0 copy-start.1
  3.0 3.1 %collective-permute-start = (f32[64,128]{1,0:T(8,128)}, f32[64,128]{1,0:T(8,128)S(1)}, u32[]{:S(2)}, u32[]{:S(2)}) collective-permute-start(f32[64,128]{1,0:T(8,128)} %bitcast.7), channel_id=1, source_target_pairs={{0,4},{1,5},{2,6},{3,7},{4,0},{5,1},{6,2},{7,3},{8,12},{9,13},{10,... | collective-permute-start | bytes 98312 | tf_op jit(solution)/shard_map/ppermute | solution.py:207
  6.1 2.6 %collective-permute-start.1 = (f32[64,128]{1,0:T(8,128)}, f32[64,128]{1,0:T(8,128)S(1)}, u32[]{:S(2)}, u32[]{:S(2)}) collective-permute-start(f32[64,128]{1,0:T(8,128)} %bitcast.8), channel_id=1, source_target_pairs={{0,8},{1,9},{2,10},{3,11},{4,12},{5,13},{6,14},{7,15},{8,0},{9,1},... | collective-permute-start | bytes 98312 | tf_op jit(solution)/shard_map/ppermute | solution.py:207
  8.7 0.0 collective-permute-start.2
  8.7 0.8 %constant_dynamic-update-slice_fusion.4 = f32[512,128]{1,0:T(8,128)S(1)} fusion(f32[64,128]{1,0:T(8,128)} %bitcast.10), kind=kLoop, calls=%fused_computation.5 | loop fusion | bytes 65536
  9.5 0.0 collective-permute-done
  9.5 2.2 %collective-permute-done.1 = f32[64,128]{1,0:T(8,128)S(1)} collective-permute-done((f32[64,128]{1,0:T(8,128)}, f32[64,128]{1,0:T(8,128)S(1)}, u32[]{:S(2)}, u32[]{:S(2)}) %collective-permute-start.1) | collective-permute-done | bytes 32800 | tf_op jit(solution)/shard_map/ppermute | solution.py:207
  11.7 2.9 %collective-permute-done.2 = f32[64,128]{1,0:T(8,128)S(1)} collective-permute-done((f32[64,128]{1,0:T(8,128)}, f32[64,128]{1,0:T(8,128)S(1)}, u32[]{:S(2)}, u32[]{:S(2)}) %collective-permute-start.2) | collective-permute-done | bytes 32800 | tf_op jit(solution)/shard_map/ppermute | solution.py:207
  14.6 0.0 copy-done.1
  14.6 1.6 %collective-permute-start.3 = (f32[256,128]{1,0:T(8,128)S(1)}, f32[256,128]{1,0:T(8,128)S(1)}, u32[]{:S(2)}, u32[]{:S(2)}) collective-permute-start(f32[256,128]{1,0:T(8,128)S(1)} %pad_maximum_fusion), channel_id=1, source_target_pairs={{0,2},{1,3},{2,0},{3,1},{4,6},{5,7},{6,4},{7,5},{8,10},{9,11},{10,... | collective-permute-start | bytes 393224 | tf_op jit(solution)/shard_map/ppermute | solution.py:207
  16.2 3.4 %collective-permute-done.3 = f32[256,128]{1,0:T(8,128)S(1)} collective-permute-done((f32[256,128]{1,0:T(8,128)S(1)}, f32[256,128]{1,0:T(8,128)S(1)}, u32[]{:S(2)}, u32[]{:S(2)}) %collective-permute-start.3) | collective-permute-done | bytes 131104 | tf_op jit(solution)/shard_map/ppermute | solution.py:207
  19.7 0.0 copy-start
  19.7 0.1 collective-permute-start.4
  19.8 1.5 %collective-permute-done.4.far = f32[512,128]{1,0:T(8,128)S(1)} collective-permute-done((f32[512,128]{1,0:T(8,128)S(1)}, f32[512,128]{1,0:T(8,128)S(1)}, u32[]{:S(2)}, u32[]{:S(2)}) %collective-permute-start.4) | collective-permute-done | bytes 262176 | tf_op jit(solution)/shard_map/ppermute | solution.py:207
  21.3 0.0 copy-start.2
  21.3 0.0 copy-done
  21.3 0.7 %copy-done.2 = f32[512,128]{1,0:T(8,128)} copy-done((f32[512,128]{1,0:T(8,128)}, f32[512,128]{1,0:T(8,128)S(1)}, u32[]{:S(2)}) %copy-start.2) | copy-done | bytes 262168
  22.0 5.5 %fit.1 = (f32[48,256]{1,0:T(8,128)}, f32[1,32]{1,0:T(1,128)}) custom-call(s32[1]{0:T(128)} %bitcast.place, f32[512,128]{1,0:T(8,128)} %copy-done, f32[512,128]{1,0:T(8,128)} %copy-done.2, f32[32,40]{1,0:T(8,128)} %systematics.1, s32[1,8]{1,0:T(1,128)} %bitcast.15), custom_call_target="tpu_custom_call" | custom-call | tf_op jit(solution)/shard_map/fit/pallas_call | solution.py:186
  27.5 1.5 %copy.9 = f32[48,1,256]{2,1,0:T(1,128)} copy(f32[48,1,256]{2,0,1:T(8,128)} %bitcast.13) | data formatting | bytes 98304
  (5 shorter events, 0.0 us)
Async XLA Ops:
  3.0 11.6 %copy-start.1 = (f32[2,2,16,128]{3,2,1,0:T(8,128)S(1)}, f32[2,2,16,128]{3,2,1,0:T(8,128)}, u32[]{:S(2)}) copy-start(f32[2,2,16,128]{3,2,1,0:T(8,128)} %subtract.1) | copy-start | bytes 98308
  3.0 6.5 %collective-permute-start = (f32[64,128]{1,0:T(8,128)}, f32[64,128]{1,0:T(8,128)S(1)}, u32[]{:S(2)}, u32[]{:S(2)}) collective-permute-start(f32[64,128]{1,0:T(8,128)} %bitcast.7), channel_id=1, source_target_pairs={{0,4},{1,5},{2,6},{3,7},{4,0},{5,1},{6,2},{7,3},{8,12},{9,13},{10,... | collective-permute-start | bytes 98312 | tf_op jit(solution)/shard_map/ppermute | solution.py:207
  6.1 5.6 %collective-permute-start.1 = (f32[64,128]{1,0:T(8,128)}, f32[64,128]{1,0:T(8,128)S(1)}, u32[]{:S(2)}, u32[]{:S(2)}) collective-permute-start(f32[64,128]{1,0:T(8,128)} %bitcast.8), channel_id=1, source_target_pairs={{0,8},{1,9},{2,10},{3,11},{4,12},{5,13},{6,14},{7,15},{8,0},{9,1},... | collective-permute-start | bytes 98312 | tf_op jit(solution)/shard_map/ppermute | solution.py:207
  8.7 5.9 %collective-permute-start.2 = (f32[64,128]{1,0:T(8,128)}, f32[64,128]{1,0:T(8,128)S(1)}, u32[]{:S(2)}, u32[]{:S(2)}) collective-permute-start(f32[64,128]{1,0:T(8,128)} %bitcast.9), channel_id=1, source_target_pairs={{0,12},{1,13},{2,14},{3,15},{4,8},{5,9},{6,10},{7,11},{8,4},{9,5},... | collective-permute-start | bytes 98312 | tf_op jit(solution)/shard_map/ppermute | solution.py:207
  14.6 5.0 %collective-permute-start.3 = (f32[256,128]{1,0:T(8,128)S(1)}, f32[256,128]{1,0:T(8,128)S(1)}, u32[]{:S(2)}, u32[]{:S(2)}) collective-permute-start(f32[256,128]{1,0:T(8,128)S(1)} %pad_maximum_fusion), channel_id=1, source_target_pairs={{0,2},{1,3},{2,0},{3,1},{4,6},{5,7},{6,4},{7,5},{8,10},{9,11},{10,... | collective-permute-start | bytes 393224 | tf_op jit(solution)/shard_map/ppermute | solution.py:207
  19.7 1.6 %copy-start = (f32[512,128]{1,0:T(8,128)}, f32[512,128]{1,0:T(8,128)S(1)}, u32[]{:S(2)}) copy-start(f32[512,128]{1,0:T(8,128)S(1)} %constant_dynamic-update-slice_fusion.near) | copy-start | bytes 786436
  19.7 1.6 %collective-permute-start.4 = (f32[512,128]{1,0:T(8,128)S(1)}, f32[512,128]{1,0:T(8,128)S(1)}, u32[]{:S(2)}, u32[]{:S(2)}) collective-permute-start(f32[512,128]{1,0:T(8,128)S(1)} %constant_dynamic-update-slice_fusion.near), channel_id=1, source_target_pairs={{0,1},{1,0},{2,3},{3,2},{4,5},{5,4},{6,7},{7,6},{8,9},{9,8},{10,11... | collective-permute-start | bytes 786440 | tf_op jit(solution)/shard_map/ppermute | solution.py:207
  21.3 0.7 %copy-start.2 = (f32[512,128]{1,0:T(8,128)}, f32[512,128]{1,0:T(8,128)S(1)}, u32[]{:S(2)}) copy-start(f32[512,128]{1,0:T(8,128)S(1)} %collective-permute-done.4.far) | copy-start | bytes 786436
